TPU v7x, 32 devices: a whole 2x2x4 slice. The times are simulated.
32 devices in a mesh: wide: 16 (over z, x, core), narrow: 2 (over y).
Axes of the slice: x: 2, y: 2, z: 4, core: 2. Of those that a mesh axis runs over, the one named last changes fastest.
Arguments:
- vectors: float32 [1024, 16384], P('narrow', 'wide'), may hold values from -6 to 6
- weights: bfloat16 [5, 64, 256, 512], P(None, 'wide', 'narrow'), may hold values from -0.25 to 0.25
Outputs:
- transformed: float32 [1024, 16384], P('narrow', 'wide')
All inputs are finite; a program needn't handle non-finite values.
Results may differ from a plain program's by a relative error of at most 0.0003.
Values may be sent and summed in bfloat16 or wider, within the bound.
A program may use at most 64 MiB of HBM per device.

v0:
```python
import jax
import jax.numpy as jnp
from jax import lax
from jax.sharding import PartitionSpec as P


def swapped(shard, axis, apart):
    return lax.ppermute(shard, axis, [(i, i ^ 1 << apart) for i in range(lax.axis_size(axis))])


def pair_local(current, level_bit):
    columns, block_count, block_size = current.shape
    stride = 1 << level_bit
    grouped = current.reshape(columns, block_count // (2 * stride), 2, stride, block_size)
    paired = jnp.concatenate([grouped[:, :, 0], grouped[:, :, 1]], -1)
    spread = jnp.broadcast_to(
        paired[:, :, None], (columns, block_count // (2 * stride), 2, stride, 2 * block_size)
    )
    return spread.reshape(columns, block_count, 2 * block_size)


def upper_side(level_bit):
    return lax.axis_index("wide") // (1 << level_bit) % 2


def pair_wide(current, level_bit):
    partner = swapped(current, "wide", level_bit)
    upper_bit = upper_side(level_bit)
    lower_half = jnp.where(upper_bit == 1, partner, current)
    upper_half = jnp.where(upper_bit == 1, current, partner)
    return jnp.concatenate([lower_half, upper_half], -1)


def contract(paired, matrix_rows):
    return jnp.einsum(
        "cbi,boi->cbo", paired, matrix_rows.astype(jnp.float32), precision=lax.Precision.HIGHEST
    )


def gathered_level(paired, level_weight):
    return contract(paired, lax.all_gather(level_weight, "narrow", axis=1, tiled=True))


def on_device(vectors, weights):
    columns, coeffs = vectors.shape
    block_size = weights.shape[3] // 2
    current = vectors.reshape(columns, coeffs // block_size, block_size)
    wide_top = lax.axis_size("wide").bit_length() - 1
    wide_bits = [0, wide_top // 2, wide_top - 1]
    for level_index in range(5):
        if level_index < 2:
            paired = pair_local(current, level_index)
            current = gathered_level(paired, weights[level_index])
        else:
            paired = pair_wide(current, wide_bits[level_index - 2])
            current = gathered_level(paired, weights[level_index])
    return current.reshape(columns, coeffs)


def solution(mesh):
    placed = (P("narrow", "wide"), P(None, "wide", "narrow", None))
    return jax.shard_map(
        on_device, mesh=mesh, in_specs=placed, out_specs=P("narrow", "wide"), check_vma=False
    )
```

profile of v0, /device:TPU:0, one launch (start us, length us, event | category | flops | bytes accessed | tf_op | source)
XLA Modules:
  0.0 252.6 jit_solution(388550160827460083)
XLA Ops:
  6.5 3.2 %fusion.27 = (bf16[1,4,128,512]{3,2,1,0:T(8,128)(2,1)}, bf16[1,4,128,512]{3,2,1,0:T(8,128)(2,1)}, bf16[1,4,128,512]{3,2,1,0:T(8,128)(2,1)}, bf16[1,4,128,512]{3,2,1,0:T(8,128)(2,1)}, bf16[1,4,128,512]{3,2,1,0:T(8,128)(2,1)}) fusion(bf16[5,4,128,512]{3,2,1,0:T(8,128)(2,1)} %param.3), kind=kLoop, calls=%fused_computation.37 | loop fusion | bytes 5242880 | tf_op jit(solution)/shard_map/slice | solution.py:56
  10.6 3.0 %reshape_reshape.3 = f32[512,2,2,1,256]{4,2,1,0,3:T(2,128)S(1)} reshape(f32[512,1024]{1,0:T(8,128)} %param.2) | data formatting | bytes 4194304 | tf_op jit(solution)/shard_map/reshape;reshape | solution.py:14
  13.6 1.1 slice_bitcast_fusion.2
  14.7 0.7 slice_bitcast_fusion.3
  15.4 1.8 pad_maximum_fusion
  17.7 16.3 %all-gather.11.cloned.1.call-done = bf16[1,4,256,512]{3,2,1,0:T(8,128)(2,1)} async-done(((bf16[1,4,128,512]{3,2,1,0:T(8,128)(2,1)}), bf16[1,4,256,512]{3,2,1,0:T(8,128)(2,1)}) %all-gather.11.cloned.1.call-update) | async-done | bytes 1048592 | tf_op jit(solution)/shard_map/all_gather | solution.py:41
  35.2 2.3 fusion.22
  37.6 1.5 maximum_bitcast_fusion
  39.1 1.9 copy.5
  41.0 15.7 %all-gather.13.cloned.1.call-done = bf16[1,4,256,512]{3,2,1,0:T(8,128)(2,1)} async-done(((bf16[1,4,128,512]{3,2,1,0:T(8,128)(2,1)}), bf16[1,4,256,512]{3,2,1,0:T(8,128)(2,1)}) %all-gather.13.cloned.1.call-update) | async-done | bytes 1048592 | tf_op jit(solution)/shard_map/all_gather | solution.py:41
  58.0 2.3 convolution_bitcast_fusion
  60.7 4.0 %collective-permute-done = f32[512,4,256]{0,2,1:T(8,128)} collective-permute-done((f32[512,4,256]{0,2,1:T(8,128)S(1)}, f32[512,4,256]{0,2,1:T(8,128)}, u32[]{:S(2)}, u32[]{:S(2)}) %collective-permute-start) | collective-permute-done | bytes 2097184 | tf_op jit(solution)/shard_map/ppermute | solution.py:8
  64.7 4.4 %broadcast_select_fusion.1 = (f32[512,4,256]{0,2,1:T(8,128)}, f32[512,4,256]{0,2,1:T(8,128)}) fusion(f32[512,4,256]{0,2,1:T(8,128)} %collective-permute-done, f32[512,4,256]{0,2,1:T(8,128)S(1)} %convolution_bitcast_fusion, pred[]{:T(512)S(6)} %eq.18), kind=kLoop, calls=%fused_computation.29 | loop fusion | flops 1048576 | bytes 8388609 | tf_op jit(solution)/shard_map/jit(_where)/select_n | solution.py:29
  69.0 13.0 %all-gather.15.cloned.1.call-done = bf16[1,4,256,512]{3,2,1,0:T(8,128)(2,1)} async-done(((bf16[1,4,128,512]{3,2,1,0:T(8,128)(2,1)}), bf16[1,4,256,512]{3,2,1,0:T(8,128)(2,1)}) %all-gather.15.cloned.1.call-update) | async-done | bytes 1048592 | tf_op jit(solution)/shard_map/all_gather | solution.py:41
  82.0 4.6 %fusion.15 = f32[512,4,256]{0,2,1:T(8,128)S(1)} fusion(f32[512,4,256]{0,2,1:T(8,128)} %get-tuple-element.10, f32[512,4,256]{0,2,1:T(8,128)} %get-tuple-element.9, bf16[1,4,256,512]{3,2,1,0:T(8,128)(2,1)} %all-gather.15.cloned.1.call-done), kind=kOutput, calls=%fused_computation.16 | convolution fusion | flops 3222274048 | bytes 7340032 | tf_op jit(solution)/shard_map/cbi,boi->cbo/dot_general | solution.py:35
  86.6 1.6 collective-permute-start.1
  88.3 45.7 %collective-permute-done.1 = f32[512,4,256]{0,2,1:T(8,128)} collective-permute-done((f32[512,4,256]{0,2,1:T(8,128)S(1)}, f32[512,4,256]{0,2,1:T(8,128)}, u32[]{:S(2)}, u32[]{:S(2)}) %collective-permute-start.1) | collective-permute-done | bytes 2097184 | tf_op jit(solution)/shard_map/ppermute | solution.py:8
  134.0 4.4 %broadcast_select_fusion.3 = (f32[512,4,256]{0,2,1:T(8,128)}, f32[512,4,256]{0,2,1:T(8,128)}) fusion(f32[512,4,256]{0,2,1:T(8,128)} %collective-permute-done.1, f32[512,4,256]{0,2,1:T(8,128)S(1)} %fusion.15, pred[]{:T(512)S(6)} %eq.17), kind=kLoop, calls=%fused_computation.31 | loop fusion | flops 1048576 | bytes 8388609 | tf_op jit(solution)/shard_map/jit(_where)/select_n | solution.py:29
  138.3 4.6 %fusion.12 = f32[512,4,256]{0,2,1:T(8,128)S(1)} fusion(f32[512,4,256]{0,2,1:T(8,128)} %get-tuple-element.8, f32[512,4,256]{0,2,1:T(8,128)} %get-tuple-element.7, bf16[1,4,256,512]{3,2,1,0:T(8,128)(2,1)} %all-gather.17.cloned.1.call-done), kind=kOutput, calls=%fused_computation.15 | convolution fusion | flops 3222274048 | bytes 7340032 | tf_op jit(solution)/shard_map/cbi,boi->cbo/dot_general | solution.py:35
  143.0 2.5 collective-permute-start.2
  145.5 89.8 %collective-permute-done.2 = f32[512,4,256]{0,2,1:T(8,128)} collective-permute-done((f32[512,4,256]{0,2,1:T(8,128)S(1)}, f32[512,4,256]{0,2,1:T(8,128)}, u32[]{:S(2)}, u32[]{:S(2)}) %collective-permute-start.2) | collective-permute-done | bytes 2097184 | tf_op jit(solution)/shard_map/ppermute | solution.py:8
  235.3 4.4 %broadcast_select_fusion.5 = (f32[512,4,256]{0,2,1:T(8,128)}, f32[512,4,256]{0,2,1:T(8,128)}) fusion(f32[512,4,256]{0,2,1:T(8,128)} %collective-permute-done.2, f32[512,4,256]{0,2,1:T(8,128)S(1)} %fusion.12, pred[]{:T(512)S(6)} %eq.16), kind=kLoop, calls=%fused_computation.33 | loop fusion | flops 1048576 | bytes 8388609 | tf_op jit(solution)/shard_map/jit(_where)/select_n | solution.py:29
  239.7 4.6 %fusion.8 = f32[4,512,256]{1,2,0:T(8,128)S(1)} fusion(f32[512,4,256]{0,2,1:T(8,128)} %get-tuple-element.6, f32[512,4,256]{0,2,1:T(8,128)} %get-tuple-element.5, bf16[1,4,256,512]{3,2,1,0:T(8,128)(2,1)} %all-gather.19.cloned.1.call-done), kind=kOutput, calls=%fused_computation.8 | convolution fusion | flops 3222274048 | bytes 7340032 | tf_op jit(solution)/shard_map/cbi,boi->cbo/dot_general | solution.py:35
  244.3 1.8 copy.9
  (21 shorter events, 4.2 us)
Async XLA Ops:
  6.5 27.4 %all-gather.11.cloned.1.call-start = ((), (), s32[]{:S(2)}) async-start(), calls=%async_computation | async-start | bytes 1572864 | tf_op jit(solution)/shard_map/all_gather | solution.py:41
  9.8 47.0 %all-gather.13.cloned.1.call-start = ((), (), s32[]{:S(2)}) async-start(), calls=%async_computation.1 | async-start | bytes 1572864 | tf_op jit(solution)/shard_map/all_gather | solution.py:41
  10.5 71.5 %all-gather.15.cloned.1.call-start = ((), (), s32[]{:S(2)}) async-start(), calls=%async_computation.2 | async-start | bytes 1572864 | tf_op jit(solution)/shard_map/all_gather | solution.py:41
  33.9 1.2 copy-start.1
  56.8 1.2 copy-start
  60.3 4.4 %collective-permute-start = (f32[512,4,256]{0,2,1:T(8,128)S(1)}, f32[512,4,256]{0,2,1:T(8,128)}, u32[]{:S(2)}, u32[]{:S(2)}) collective-permute-start(f32[512,4,256]{0,2,1:T(8,128)S(1)} %convolution_bitcast_fusion), channel_id=1, source_target_pairs={{0,2},{2,0},{4,6},{6,4},{8,10},{10,8},{12,14},{14,12},{16,18},{18,... | collective-permute-start | bytes 6291464 | tf_op jit(solution)/shard_map/ppermute | solution.py:8
  60.4 77.9 %all-gather.17.cloned.1.call-start = ((), (), s32[]{:S(2)}) async-start(), calls=%async_computation.3 | async-start | bytes 1572864 | tf_op jit(solution)/shard_map/all_gather | solution.py:41
  86.6 47.4 %collective-permute-start.1 = (f32[512,4,256]{0,2,1:T(8,128)S(1)}, f32[512,4,256]{0,2,1:T(8,128)}, u32[]{:S(2)}, u32[]{:S(2)}) collective-permute-start(f32[512,4,256]{0,2,1:T(8,128)S(1)} %fusion.15), channel_id=1, source_target_pairs={{0,8},{2,10},{4,12},{6,14},{8,0},{10,2},{12,4},{14,6},{16,24},{18,... | collective-permute-start | bytes 6291464 | tf_op jit(solution)/shard_map/ppermute | solution.py:8
  88.2 151.5 %all-gather.19.cloned.1.call-start = ((), (), s32[]{:S(2)}) async-start(), calls=%async_computation.4 | async-start | bytes 1572864 | tf_op jit(solution)/shard_map/all_gather | solution.py:41
  143.0 92.4 %collective-permute-start.2 = (f32[512,4,256]{0,2,1:T(8,128)S(1)}, f32[512,4,256]{0,2,1:T(8,128)}, u32[]{:S(2)}, u32[]{:S(2)}) collective-permute-start(f32[512,4,256]{0,2,1:T(8,128)S(1)} %fusion.12), channel_id=1, source_target_pairs={{0,16},{2,18},{4,20},{6,22},{8,24},{10,26},{12,28},{14,30},{16,0},... | collective-permute-start | bytes 6291464 | tf_op jit(solution)/shard_map/ppermute | solution.py:8
Sparse Core Ops, SparseCore 0:
  9.9 23.9 all-gather.10
  35.5 21.2 all-gather.12
  60.5 21.4 all-gather.14
  88.3 20.3 all-gather.16
  145.6 19.4 all-gather.18
where the time goes:
time: 253 us
  waiting for transfers between devices  185 us (73%)
  matrix products  18.4 us (7%)
  other arithmetic  16.3 us (6%)
  local copies, waits for them, and re-layouts  14.8 us (6%)
  between operations  13.3 us (5%)
  starting transfers between devices  4.44 us (2%)
    ppermute x3, waiting for transfers between devices, swapped(): lax.ppermute(shard, axis, [(i, i ^ 1 << apart) for i in range(lax.axis_si...  140 us
    all_gather x5, waiting for transfers between devices, gathered_level(): lax.all_gather(level_weight, 'narrow', axis=1, tiled=True)  45 us
    dot_general x5, matrix products, contract(): jnp.einsum('cbi,boi->cbo', paired, matrix_rows.astype(jnp.float32), preci...  18.4 us
    select_n x3, other arithmetic, pair_wide(): lower_half = jnp.where(upper_bit == 1, partner, current)  13.1 us
  transfers between devices with their start and end apart: 8, of which 6 were waited for; matrix products, arithmetic and copies ran while one was open for 11% of the time, Pallas kernels for 0%

commit v1 on v0

--- a/solution.py
+++ b/solution.py
@@ -2,6 +2,13 @@
 import jax.numpy as jnp
 from jax import lax
 from jax.sharding import PartitionSpec as P
+
+
+def expand_forms(mat):
+    x_now = jax.lax.all_to_all(
+        jnp.stack(tuple((mat for _ in range(jax.lax.psum(1, "narrow"))))), "narrow", 0, 0
+    )
+    return jnp.concatenate(x_now, axis=1)
 
 
 def swapped(shard, axis, apart):
@@ -38,7 +45,7 @@
 
 
 def gathered_level(paired, level_weight):
-    return contract(paired, lax.all_gather(level_weight, "narrow", axis=1, tiled=True))
+    return contract(paired, expand_forms(level_weight))
 
 
 def on_device(vectors, weights):

time: 253 us -> 219 us (0.87)
  waiting for transfers between devices: 185 us -> 152 us
  starting transfers between devices: 4.44 us -> 23 us
  between operations: 13.3 us -> 0.33 us
  matrix products: 18.4 us -> 10.8 us
    all_to_all x0 -> x5, waiting for transfers between devices: none -> 51.6 us  [expand_forms(): jax.lax.all_to_all(jnp.stack(tuple((mat for _ in range(jax.lax.psum(1, 'n...]
    all_gather x5 -> x0, waiting for transfers between devices: 45 us -> none  [gathered_level(): lax.all_gather(level_weight, 'narrow', axis=1, tiled=True)]
    ppermute x3, waiting for transfers between devices: 140 us -> 100 us  [swapped(): lax.ppermute(shard, axis, [(i, i ^ 1 << apart) for i in range(lax.axis_si...]
    all_to_all x0 -> x5, starting transfers between devices: none -> 18.8 us  [expand_forms(): jax.lax.all_to_all(jnp.stack(tuple((mat for _ in range(jax.lax.psum(1, 'n...]
    dot_general x5, matrix products: 18.4 us -> 10.8 us  [contract(): jnp.einsum('cbi,boi->cbo', paired, matrix_rows.astype(jnp.float32), preci...]
    select_n x3, other arithmetic: 13.1 us -> 6.77 us  [pair_wide(): lower_half = jnp.where(upper_bit == 1, partner, current)]
    another operation x0 -> x5, other arithmetic: none -> 5.31 us  [expand_forms(): jnp.stack(tuple((mat for _ in range(jax.lax.psum(1, 'narrow')))))]
  transfers between devices with their start and end apart: 8 -> 8, of which waited for: 6 -> 7; matrix products, arithmetic and copies ran while one was open for 11% -> 9% of each run, Pallas kernels for 0% -> 0%
where the time goes in v1:
time: 219 us; the launch traced here: 218 us
  waiting for transfers between devices  152 us (69%)
  starting transfers between devices  23 us (11%)
  local copies, waits for them, and re-layouts  16.5 us (8%)
  other arithmetic  15.4 us (7%)
  matrix products  10.8 us (5%)
    ppermute x3, waiting for transfers between devices, swapped(): lax.ppermute(shard, axis, [(i, i ^ 1 << apart) for i in range(lax.axis_si...  100 us
    all_to_all x5, waiting for transfers between devices, expand_forms(): jax.lax.all_to_all(jnp.stack(tuple((mat for _ in range(jax.lax.psum(1, 'n...  51.6 us
    all_to_all x5, starting transfers between devices, expand_forms(): jax.lax.all_to_all(jnp.stack(tuple((mat for _ in range(jax.lax.psum(1, 'n...  18.8 us
    dot_general x5, matrix products, contract(): jnp.einsum('cbi,boi->cbo', paired, matrix_rows.astype(jnp.float32), preci...  10.8 us
    select_n x3, other arithmetic, pair_wide(): lower_half = jnp.where(upper_bit == 1, partner, current)  6.77 us
    another operation x5, other arithmetic, expand_forms(): jnp.stack(tuple((mat for _ in range(jax.lax.psum(1, 'narrow')))))  5.31 us
  transfers between devices with their start and end apart: 8, of which 7 were waited for; matrix products, arithmetic and copies ran while one was open for 9% of the time, Pallas kernels for 0%

profile of v1, /device:TPU:0, one launch (start us, length us, event | category | flops | bytes accessed | tf_op | source)
XLA Modules:
  0.0 217.8 jit_solution(12329616684793876451)
XLA Ops:
  0.0 3.1 %fusion.21 = (bf16[1,4,128,512]{3,2,1,0:T(8,128)(2,1)S(1)}, bf16[1,4,128,512]{3,2,1,0:T(8,128)(2,1)}, bf16[1,4,128,512]{3,2,1,0:T(8,128)(2,1)}, bf16[1,4,128,512]{3,2,1,0:T(8,128)(2,1)}, bf16[1,4,128,512]{3,2,1,0:T(8,128)(2,1)}) fusion(bf16[5,4,128,512]{3,2,1,0:T(8,128)(2,1)} %param.3), kind=kLoop, calls=%fused_computation.36 | loop fusion | bytes 5242880 | tf_op jit(solution)/shard_map/slice | solution.py:60
  4.1 4.3 %all-to-all-start.4 = ((bf16[2,4,128,512]{3,2,1,0:T(8,128)(2,1)}), bf16[2,4,128,512]{3,2,1,0:T(8,128)(2,1)S(1)}, u32[]{:S(2)}, u32[]{:S(2)}) async-start(bf16[2,4,128,512]{3,2,1,0:T(8,128)(2,1)} %pad_maximum_fusion.5), calls=%async_computation.4 | async-start | bytes 2097152 | tf_op jit(solution)/shard_map/all_to_all | solution.py:8
  8.4 3.0 %reshape_reshape.3 = f32[512,2,2,1,256]{4,2,1,0,3:T(2,128)S(1)} reshape(f32[512,1024]{1,0:T(8,128)} %param.2) | data formatting | bytes 4194304 | tf_op jit(solution)/shard_map/reshape;reshape | solution.py:21
  17.2 5.6 %all-to-all-done.4 = bf16[2,4,128,512]{3,2,1,0:T(8,128)(2,1)S(1)} async-done(((bf16[2,4,128,512]{3,2,1,0:T(8,128)(2,1)}), bf16[2,4,128,512]{3,2,1,0:T(8,128)(2,1)S(1)}, u32[]{:S(2)}, u32[]{:S(2)}) %all-to-all-start.4) | async-done | bytes 1048608 | tf_op jit(solution)/shard_map/all_to_all | solution.py:8
  23.8 3.6 %all-to-all-start.3 = ((bf16[2,4,128,512]{3,2,1,0:T(8,128)(2,1)}), bf16[2,4,128,512]{3,2,1,0:T(8,128)(2,1)S(1)}, u32[]{:S(2)}, u32[]{:S(2)}) async-start(bf16[2,4,128,512]{3,2,1,0:T(8,128)(2,1)} %pad_maximum_fusion.4), calls=%async_computation.3 | async-start | bytes 2097152 | tf_op jit(solution)/shard_map/all_to_all | solution.py:8
  29.2 2.2 fusion.22
  33.1 1.9 copy.10
  35.0 5.7 %all-to-all-done.3 = bf16[2,4,128,512]{3,2,1,0:T(8,128)(2,1)S(1)} async-done(((bf16[2,4,128,512]{3,2,1,0:T(8,128)(2,1)}), bf16[2,4,128,512]{3,2,1,0:T(8,128)(2,1)S(1)}, u32[]{:S(2)}, u32[]{:S(2)}) %all-to-all-start.3) | async-done | bytes 1048608 | tf_op jit(solution)/shard_map/all_to_all | solution.py:8
  41.3 2.1 convolution_bitcast_fusion
  44.6 3.8 %all-to-all-start.2 = ((bf16[2,4,128,512]{3,2,1,0:T(8,128)(2,1)}), bf16[2,4,128,512]{3,2,1,0:T(8,128)(2,1)S(1)}, u32[]{:S(2)}, u32[]{:S(2)}) async-start(bf16[2,4,128,512]{3,2,1,0:T(8,128)(2,1)} %pad_maximum_fusion.3), calls=%async_computation.2 | async-start | bytes 2097152 | tf_op jit(solution)/shard_map/all_to_all | solution.py:8
  48.4 14.5 %all-to-all-done.2 = bf16[2,4,128,512]{3,2,1,0:T(8,128)(2,1)S(1)} async-done(((bf16[2,4,128,512]{3,2,1,0:T(8,128)(2,1)}), bf16[2,4,128,512]{3,2,1,0:T(8,128)(2,1)S(1)}, u32[]{:S(2)}, u32[]{:S(2)}) %all-to-all-start.2) | async-done | bytes 1048608 | tf_op jit(solution)/shard_map/all_to_all | solution.py:8
  63.0 2.3 %broadcast_select_fusion.1 = (f32[512,4,256]{0,2,1:T(8,128)S(1)}, f32[512,4,256]{0,2,1:T(8,128)S(1)}) fusion(f32[512,4,256]{0,2,1:T(8,128)} %collective-permute-done, f32[512,4,256]{0,2,1:T(8,128)S(1)} %convolution_bitcast_fusion, pred[]{:T(512)S(6)} %eq.18), kind=kLoop, calls=%fused_computation.28 | loop fusion | flops 1048576 | bytes 8388609 | tf_op jit(solution)/shard_map/jit(_where)/select_n | solution.py:36
  65.3 2.2 fusion.15
  70.1 3.6 %all-to-all-start.1 = ((bf16[2,4,128,512]{3,2,1,0:T(8,128)(2,1)}), bf16[2,4,128,512]{3,2,1,0:T(8,128)(2,1)S(1)}, u32[]{:S(2)}, u32[]{:S(2)}) async-start(bf16[2,4,128,512]{3,2,1,0:T(8,128)(2,1)} %pad_maximum_fusion.2), calls=%async_computation.1 | async-start | bytes 2097152 | tf_op jit(solution)/shard_map/all_to_all | solution.py:8
  73.7 13.3 %all-to-all-done.1 = bf16[2,4,128,512]{3,2,1,0:T(8,128)(2,1)S(1)} async-done(((bf16[2,4,128,512]{3,2,1,0:T(8,128)(2,1)}), bf16[2,4,128,512]{3,2,1,0:T(8,128)(2,1)S(1)}, u32[]{:S(2)}, u32[]{:S(2)}) %all-to-all-start.1) | async-done | bytes 1048608 | tf_op jit(solution)/shard_map/all_to_all | solution.py:8
  87.1 27.7 %collective-permute-done.1 = f32[512,4,256]{0,2,1:T(8,128)} collective-permute-done((f32[512,4,256]{0,2,1:T(8,128)S(1)}, f32[512,4,256]{0,2,1:T(8,128)}, u32[]{:S(2)}, u32[]{:S(2)}) %collective-permute-start.1) | collective-permute-done | bytes 2097184 | tf_op jit(solution)/shard_map/ppermute | solution.py:15
  114.8 2.3 %broadcast_select_fusion.3 = (f32[512,4,256]{0,2,1:T(8,128)S(1)}, f32[512,4,256]{0,2,1:T(8,128)S(1)}) fusion(f32[512,4,256]{0,2,1:T(8,128)} %collective-permute-done.1, f32[512,4,256]{0,2,1:T(8,128)S(1)} %fusion.15, pred[]{:T(512)S(6)} %eq.17), kind=kLoop, calls=%fused_computation.30 | loop fusion | flops 1048576 | bytes 8388609 | tf_op jit(solution)/shard_map/jit(_where)/select_n | solution.py:36
  117.0 2.2 fusion.12
  119.2 2.6 %collective-permute-start.2 = (f32[512,4,256]{0,2,1:T(8,128)S(1)}, f32[512,4,256]{0,2,1:T(8,128)}, u32[]{:S(2)}, u32[]{:S(2)}) collective-permute-start(f32[512,4,256]{0,2,1:T(8,128)S(1)} %fusion.12), channel_id=1, source_target_pairs={{0,16},{2,18},{4,20},{6,22},{8,24},{10,26},{12,28},{14,30},{16,0},... | collective-permute-start | bytes 6291464 | tf_op jit(solution)/shard_map/ppermute | solution.py:15
  122.9 3.6 %all-to-all-start = ((bf16[2,4,128,512]{3,2,1,0:T(8,128)(2,1)}), bf16[2,4,128,512]{3,2,1,0:T(8,128)(2,1)S(1)}, u32[]{:S(2)}, u32[]{:S(2)}) async-start(bf16[2,4,128,512]{3,2,1,0:T(8,128)(2,1)} %pad_maximum_fusion.1), calls=%async_computation | async-start | bytes 2097152 | tf_op jit(solution)/shard_map/all_to_all | solution.py:8
  126.5 12.5 %all-to-all-done = bf16[2,4,128,512]{3,2,1,0:T(8,128)(2,1)S(1)} async-done(((bf16[2,4,128,512]{3,2,1,0:T(8,128)(2,1)}), bf16[2,4,128,512]{3,2,1,0:T(8,128)(2,1)S(1)}, u32[]{:S(2)}, u32[]{:S(2)}) %all-to-all-start) | async-done | bytes 1048608 | tf_op jit(solution)/shard_map/all_to_all | solution.py:8
  139.0 72.5 %collective-permute-done.2 = f32[512,4,256]{0,2,1:T(8,128)} collective-permute-done((f32[512,4,256]{0,2,1:T(8,128)S(1)}, f32[512,4,256]{0,2,1:T(8,128)}, u32[]{:S(2)}, u32[]{:S(2)}) %collective-permute-start.2) | collective-permute-done | bytes 2097184 | tf_op jit(solution)/shard_map/ppermute | solution.py:15
  211.5 2.3 %broadcast_select_fusion.5 = (f32[512,4,256]{0,2,1:T(8,128)S(1)}, f32[512,4,256]{0,2,1:T(8,128)S(1)}) fusion(f32[512,4,256]{0,2,1:T(8,128)} %collective-permute-done.2, f32[512,4,256]{0,2,1:T(8,128)S(1)} %fusion.12, pred[]{:T(512)S(6)} %eq.16), kind=kLoop, calls=%fused_computation.32 | loop fusion | flops 1048576 | bytes 8388609 | tf_op jit(solution)/shard_map/jit(_where)/select_n | solution.py:36
  213.8 2.2 fusion.8
  (32 shorter events, 18.7 us)
Async XLA Ops:
  4.1 18.7 %all-to-all-start.4 = ((bf16[2,4,128,512]{3,2,1,0:T(8,128)(2,1)}), bf16[2,4,128,512]{3,2,1,0:T(8,128)(2,1)S(1)}, u32[]{:S(2)}, u32[]{:S(2)}) async-start(bf16[2,4,128,512]{3,2,1,0:T(8,128)(2,1)} %pad_maximum_fusion.5), calls=%async_computation.4 | async-start | bytes 2097152 | tf_op jit(solution)/shard_map/all_to_all | solution.py:8
  15.1 1.0 copy-start.4
  22.8 1.0 copy-start
  23.8 16.9 %all-to-all-start.3 = ((bf16[2,4,128,512]{3,2,1,0:T(8,128)(2,1)}), bf16[2,4,128,512]{3,2,1,0:T(8,128)(2,1)S(1)}, u32[]{:S(2)}, u32[]{:S(2)}) async-start(bf16[2,4,128,512]{3,2,1,0:T(8,128)(2,1)} %pad_maximum_fusion.4), calls=%async_computation.3 | async-start | bytes 2097152 | tf_op jit(solution)/shard_map/all_to_all | solution.py:8
  41.3 2.2 %copy-start.3 = (bf16[1,4,128,512]{3,2,1,0:T(8,128)(2,1)S(1)}, bf16[1,4,128,512]{3,2,1,0:T(8,128)(2,1)}, u32[]{:S(2)}) copy-start(bf16[1,4,128,512]{3,2,1,0:T(8,128)(2,1)} %get-tuple-element.12) | copy-start | bytes 1572868
  43.5 19.5 %collective-permute-start = (f32[512,4,256]{0,2,1:T(8,128)S(1)}, f32[512,4,256]{0,2,1:T(8,128)}, u32[]{:S(2)}, u32[]{:S(2)}) collective-permute-start(f32[512,4,256]{0,2,1:T(8,128)S(1)} %convolution_bitcast_fusion), channel_id=1, source_target_pairs={{0,2},{2,0},{4,6},{6,4},{8,10},{10,8},{12,14},{14,12},{16,18},{18,... | collective-permute-start | bytes 6291464 | tf_op jit(solution)/shard_map/ppermute | solution.py:15
  44.6 18.3 %all-to-all-start.2 = ((bf16[2,4,128,512]{3,2,1,0:T(8,128)(2,1)}), bf16[2,4,128,512]{3,2,1,0:T(8,128)(2,1)S(1)}, u32[]{:S(2)}, u32[]{:S(2)}) async-start(bf16[2,4,128,512]{3,2,1,0:T(8,128)(2,1)} %pad_maximum_fusion.3), calls=%async_computation.2 | async-start | bytes 2097152 | tf_op jit(solution)/shard_map/all_to_all | solution.py:8
  65.2 3.8 %copy-start.2 = (bf16[1,4,128,512]{3,2,1,0:T(8,128)(2,1)S(1)}, bf16[1,4,128,512]{3,2,1,0:T(8,128)(2,1)}, u32[]{:S(2)}) copy-start(bf16[1,4,128,512]{3,2,1,0:T(8,128)(2,1)} %get-tuple-element.13) | copy-start | bytes 1572868
  67.4 47.3 %collective-permute-start.1 = (f32[512,4,256]{0,2,1:T(8,128)S(1)}, f32[512,4,256]{0,2,1:T(8,128)}, u32[]{:S(2)}, u32[]{:S(2)}) collective-permute-start(f32[512,4,256]{0,2,1:T(8,128)S(1)} %fusion.15), channel_id=1, source_target_pairs={{0,8},{2,10},{4,12},{6,14},{8,0},{10,2},{12,4},{14,6},{16,24},{18,... | collective-permute-start | bytes 6291464 | tf_op jit(solution)/shard_map/ppermute | solution.py:15
  70.1 17.0 %all-to-all-start.1 = ((bf16[2,4,128,512]{3,2,1,0:T(8,128)(2,1)}), bf16[2,4,128,512]{3,2,1,0:T(8,128)(2,1)S(1)}, u32[]{:S(2)}, u32[]{:S(2)}) async-start(bf16[2,4,128,512]{3,2,1,0:T(8,128)(2,1)} %pad_maximum_fusion.2), calls=%async_computation.1 | async-start | bytes 2097152 | tf_op jit(solution)/shard_map/all_to_all | solution.py:8
  117.0 4.8 %copy-start.1 = (bf16[1,4,128,512]{3,2,1,0:T(8,128)(2,1)S(1)}, bf16[1,4,128,512]{3,2,1,0:T(8,128)(2,1)}, u32[]{:S(2)}) copy-start(bf16[1,4,128,512]{3,2,1,0:T(8,128)(2,1)} %get-tuple-element.14) | copy-start | bytes 1572868
  119.2 92.3 %collective-permute-start.2 = (f32[512,4,256]{0,2,1:T(8,128)S(1)}, f32[512,4,256]{0,2,1:T(8,128)}, u32[]{:S(2)}, u32[]{:S(2)}) collective-permute-start(f32[512,4,256]{0,2,1:T(8,128)S(1)} %fusion.12), channel_id=1, source_target_pairs={{0,16},{2,18},{4,20},{6,22},{8,24},{10,26},{12,28},{14,30},{16,0},... | collective-permute-start | bytes 6291464 | tf_op jit(solution)/shard_map/ppermute | solution.py:15
  122.9 16.1 %all-to-all-start = ((bf16[2,4,128,512]{3,2,1,0:T(8,128)(2,1)}), bf16[2,4,128,512]{3,2,1,0:T(8,128)(2,1)S(1)}, u32[]{:S(2)}, u32[]{:S(2)}) async-start(bf16[2,4,128,512]{3,2,1,0:T(8,128)(2,1)} %pad_maximum_fusion.1), calls=%async_computation | async-start | bytes 2097152 | tf_op jit(solution)/shard_map/all_to_all | solution.py:8
